TPU v7x, 128 devices: a whole 4x4x4 slice. The times are simulated.
128 devices in a mesh: gx: 8 (over x_lo, y), gy: 4 (over z), gz: 4 (over x_hi, core).
Axes of the slice: x: 4 (x_hi: 2, x_lo: 2; x = x_hi * 2 + x_lo), y: 4, z: 4, core: 2. Of those that a mesh axis runs over, the one named last changes fastest.
Arguments:
- gas_temp: float32 [128, 512, 1024], P('gz', 'gx', 'gy'), may hold values from 1 to 8
- fuel_frac: float32 [128, 512, 1024], P('gz', 'gx', 'gy'), may hold values from 0 to 1
- velocity: float32 [3, 128, 512, 1024], P(None, 'gz', 'gx', 'gy'), may hold values from -3 to 3
- wall_flags: int32 [512, 1024], P('gx', 'gy'), may hold values 0 or 1
- solid_temp: float32 [64, 1024, 2048], P(None, ('gx', 'gy'), 'gz'), may hold values from 1 to 3
- diffusivity: float32 [64, 1024, 2048], P(None, ('gx', 'gy'), 'gz'), may hold values from 0.03 to 0.15
- gas_owner: int32 [1024, 2048], P(('gx', 'gy'), 'gz'), may hold values from 0 to 524287, as said below
Outputs:
- gas_temp_new: float32 [128, 512, 1024], P('gz', 'gx', 'gy')
- fuel_frac_new: float32 [128, 512, 1024], P('gz', 'gx', 'gy')
- solid_temp_new: float32 [64, 1024, 2048], P(None, ('gx', 'gy'), 'gz')
Inputs may be any that keep to these rules, and one draw needn't show every extreme that they name: gas_owner[p, q] = a * 1024 + b where a differs from p // 2 by at most 4 modulo 512 and b differs from q // 2 by at most 4 modulo 1024; both offsets reach 4 in both directions.
All inputs are finite; a program needn't handle non-finite values. No bound on the sum of `wall_flags` on one device may be relied on, other than what follows from the above.
Results may differ from a plain program's by a relative error of at most 0.00002.
Values sent between devices are 32-bit elements; how exact they have to be, the bound alone decides.
A program may use at most 128 MiB of HBM per device.

v0:
```python
import functools

import jax
import jax.numpy as jnp
from jax import lax
from jax.experimental import pallas as pl
from jax.experimental.pallas import tpu as pltpu
from jax.sharding import PartitionSpec as P

MESH = pl.DeviceIdType.MESH
F32 = jnp.float32
I32 = jnp.int32

STEPS = 4
CHUNKS = 4
CL = 16
NL = 64
GL = 32
DISP = 4

PIECES = ((0, 0), (1, 1), (2, -1))
PARTS = (0, 1, 2)


def lane_iota(rows):
    return lax.broadcasted_iota(I32, (rows, 128), 1)


def local(src, dst, sem):
    copy = pltpu.make_async_copy(src, dst, sem)
    copy.start()
    return copy


def kernel(
    gas_ref, fuel_ref, vel_ref, flags_ref, solid_ref, diff_ref, owner_ref,
    gas_out, fuel_out, solid_out,
    G, V, S, D, FL, OW, FS, FB, U, FX,
    WRs, WRr, WCs, WCr, GRs, GRr, GCs, GCr, T0, WTs, WTr,
    lsem, w_send, w_recv, g_send, g_recv, f_send, f_recv, t_send, t_recv,
):
    gx, gy, gz = lax.axis_index("gx"), lax.axis_index("gy"), lax.axis_index("gz")
    row = gx * 4 + gy

    def row_device(r):
        r = lax.rem(r + 32, 32)
        return (lax.div(r, 4), lax.rem(r, 4), gz)

    up_dev = row_device(row - 1)
    down_dev = row_device(row + 1)
    left_dev = (gx, gy, lax.rem(gz + 3, 4))
    right_dev = (gx, gy, lax.rem(gz + 1, 4))
    xm = lax.rem(gx + 7, 8)
    xp = lax.rem(gx + 1, 8)
    gxm_dev = (xm, gy, gz)
    gxp_dev = (xp, gy, gz)
    gym_dev = (gx, lax.rem(gy + 3, 4), gz)
    gyp_dev = (gx, lax.rem(gy + 1, 4), gz)

    loads = {}
    n = 0
    for j in range(2):
        loads["g0", j] = local(
            gas_ref.at[:, :, pl.ds(128 * j, 128)], G.at[0, pl.ds(1, GL), j, pl.ds(8, 64), :], lsem.at[n]
        )
        n += 1
    loads["fl"] = local(flags_ref, FL, lsem.at[n])
    n += 1
    for j in range(4):
        loads["s", j] = local(
            solid_ref.at[:, :, pl.ds(128 * j, 128)], S.at[0, pl.ds(0, NL), j, pl.ds(8, 32), :], lsem.at[n]
        )
        n += 1
    for j in range(2):
        loads["g1", j] = local(
            fuel_ref.at[:, :, pl.ds(128 * j, 128)], G.at[1, pl.ds(1, GL), j, pl.ds(8, 64), :], lsem.at[n]
        )
        n += 1
    loads["ow"] = local(owner_ref, OW, lsem.at[n])
    n += 1
    loads["v"] = local(vel_ref, V, lsem.at[n])
    n += 1
    loads["d"] = local(diff_ref, D, lsem.at[n])

    barrier = pltpu.get_barrier_semaphore()

    def greet(dev):
        pl.semaphore_signal(barrier, inc=1, device_id=dev, device_id_type=MESH)

    for dev in (up_dev, down_dev, left_dev, right_dev, gxm_dev, gxp_dev, gym_dev, gyp_dev):
        greet(dev)
    at_wall = gz == 0
    at_top = gz == 3

    def is_me(a, b, c):
        return (a == gx) & (b == gy) & (c == gz)

    def face_targets():
        out = []
        for piece, shift in PIECES:
            tz = lax.rem(gy + shift + 4, 4)
            for t in range(4):
                self_ = (t == gy) & (tz == 0)
                out.append(((gx, t, tz), piece, 1, 16 * t, self_))
                if t > 0:
                    out.append(((gx, t, tz), piece, 0, 16 * t - 8, self_))
                if t < 3:
                    out.append(((gx, t, tz), piece, 2, 16 * t + 16, self_))
            out.append(((xp, 0, tz), piece, 0, 56, None))
            out.append(((xm, 3, tz), piece, 2, 0, None))
        return out

    def face_devices():
        out = []
        for piece, shift in PIECES:
            tz = lax.rem(gy + shift + 4, 4)
            for t in range(4):
                out.append(((gx, t, tz), (t == gy) & (tz == 0)))
            out.append(((xp, 0, tz), None))
            out.append(((xm, 3, tz), None))
        return out

    count = I32(8)

    @pl.when(at_wall)
    def _():
        for dev, self_ in face_devices():
            if self_ is None:
                greet(dev)
            else:
                pl.when(jnp.logical_not(self_))(functools.partial(greet, dev))

    sources = []
    for piece, shift in PIECES:
        sy = lax.rem(gz - shift + 4, 4)
        self_ = (gz == 0) & (sy == gy)
        sources.append(((gx, sy, 0), self_))
        pl.when(jnp.logical_not(self_))(functools.partial(greet, (gx, sy, 0)))
        pl.when(gy == 0)(functools.partial(greet, (xm, sy, 0)))
        pl.when(gy == 3)(functools.partial(greet, (xp, sy, 0)))
        other = jnp.where(self_, 0, 1) + jnp.where((gy == 0) | (gy == 3), 1, 0)
        count = count + other
    self_sends = I32(0)
    for _, self_ in face_devices():
        if self_ is not None:
            self_sends = self_sends + jnp.where(self_, 1, 0)
    count = count + jnp.where(at_wall, 18 - self_sends, 0)

    S[0, NL] = jnp.ones((4, 48, 128), F32)
    S[1, NL] = jnp.ones((4, 48, 128), F32)

    def send(src, dst, ssem, rsem, dev):
        return pltpu.make_async_remote_copy(
            src_ref=src, dst_ref=dst, send_sem=ssem, recv_sem=rsem, device_id=dev, device_id_type=MESH
        )

    def wall_copies(s, c):
        rows = pl.ds(CL * c, CL)
        return (
            send(WRs.at[s, 0, :, rows, :], WRr.at[s, 1, :, rows, :], w_send.at[s, c, 0], w_recv.at[s, c, 1], up_dev),
            send(WRs.at[s, 1, :, rows, :], WRr.at[s, 0, :, rows, :], w_send.at[s, c, 1], w_recv.at[s, c, 0], down_dev),
            send(WCs.at[s, 0, c], WCr.at[s, 1, c], w_send.at[s, c, 2], w_recv.at[s, c, 3], left_dev),
            send(WCs.at[s, 1, c], WCr.at[s, 0, c], w_send.at[s, c, 3], w_recv.at[s, c, 2], right_dev),
        )

    lane32 = lane_iota(32)
    lane64 = lane_iota(64)

    for j in range(4):
        loads["s", j].wait()

    for c in range(CHUNKS):
        def pack(i, carry, c=c):
            cl, cr = carry
            l = CL * c + i
            for j in range(4):
                WRs[0, 0, j, pl.ds(l, 1), :] = S[0, l, j, 8:9, :]
                WRs[0, 1, j, pl.ds(l, 1), :] = S[0, l, j, 39:40, :]
            cl = jnp.where(lane32 == i, pltpu.roll(S[0, l, 0, 8:40, :], i, 1), cl)
            cr = jnp.where(lane32 == i, pltpu.roll(S[0, l, 3, 8:40, :], i + 1, 1), cr)
            return cl, cr

        zero = jnp.zeros((32, 128), F32)
        cl, cr = lax.fori_loop(0, CL, pack, (zero, zero))
        WCs[0, 0, c] = cl
        WCs[0, 1, c] = cr

    for key in (("g0", 0), ("g0", 1), "fl", ("g1", 0), ("g1", 1)):
        loads[key].wait()
    for j in range(2):
        FS[0, j] = G[0, 1, j, 8:72, :]
        FS[1, j] = FL[:, 128 * j : 128 * j + 128].astype(F32)

    def gpack(l, carry):
        cl, cr = carry
        for f in range(2):
            for j in range(2):
                GRs[0, f, j, pl.ds(l, 1), :] = G[f, l + 1, j, 8:9, :]
                GRs[1, f, j, pl.ds(l, 1), :] = G[f, l + 1, j, 71:72, :]
            i = f * GL + l
            cl = jnp.where(lane64 == i, pltpu.roll(G[f, l + 1, 0, 8:72, :], i, 1), cl)
            cr = jnp.where(lane64 == i, pltpu.roll(G[f, l + 1, 1, 8:72, :], i + 1, 1), cr)
        return cl, cr

    zero = jnp.zeros((64, 128), F32)
    cl, cr = lax.fori_loop(0, GL, gpack, (zero, zero))
    GCs[0] = cl
    GCs[1] = cr

    pl.semaphore_wait(barrier, count)

    for c in reversed(range(CHUNKS)):
        for copy in wall_copies(0, c):
            copy.start()

    def face_ref(buf, piece):
        return buf.at[:, pl.ds(1, 2)] if piece == 0 else buf.at[:, pl.ds(0 if piece == 1 else 3, 1)]

    def face_source(piece):
        return FS if piece == 0 else FS.at[:, pl.ds(1 if piece == 1 else 0, 1)]

    PART = ((0, 8), (8, 16), (24, 8))

    def face_copy(n, dev, piece, part, r):
        start, size = PART[part]
        return send(
            face_source(piece).at[:, :, pl.ds(r, size), :],
            face_ref(FB, piece).at[:, :, pl.ds(start, size), :],
            f_send.at[n],
            f_recv.at[piece, part],
            dev,
        )

    def face_here(piece, part, r):
        start, size = PART[part]
        if piece == 0:
            FB[:, 1:3, start : start + size, :] = FS[:, :, r : r + size, :]
        elif piece == 1:
            FB[:, 0, start : start + size, :] = FS[:, 1, r : r + size, :]
        else:
            FB[:, 3, start : start + size, :] = FS[:, 0, r : r + size, :]

    @pl.when(at_wall)
    def _():
        for n, (dev, piece, part, r, self_) in enumerate(face_targets()):
            copy = face_copy(n, dev, piece, part, r)
            if self_ is None:
                copy.start()
            else:
                pl.when(jnp.logical_not(self_))(copy.start)
                pl.when(self_)(functools.partial(face_here, piece, part, r))

    g_copies = (
        send(GRs.at[0], GRr.at[1], g_send.at[0], g_recv.at[1], gxm_dev),
        send(GRs.at[1], GRr.at[0], g_send.at[1], g_recv.at[0], gxp_dev),
        send(GCs.at[0], GCr.at[1], g_send.at[2], g_recv.at[3], gym_dev),
        send(GCs.at[1], GCr.at[0], g_send.at[3], g_recv.at[2], gyp_dev),
    )
    for copy in g_copies:
        copy.start()
    z_down = send(
        G.at[:, 1, :, pl.ds(8, 64), :], G.at[:, GL + 1, :, pl.ds(8, 64), :], g_send.at[4], g_recv.at[5], left_dev
    )
    z_up = send(
        G.at[:, GL, :, pl.ds(8, 64), :], G.at[:, 0, :, pl.ds(8, 64), :], g_send.at[5], g_recv.at[4], right_dev
    )
    pl.when(jnp.logical_not(at_wall))(z_down.start)
    pl.when(jnp.logical_not(at_top))(z_up.start)

    def gas_layer(l):
        g = l + 1
        for f in range(2):
            for j in range(2):
                G[f, g, j, 7:8, :] = GRr[0, f, j, pl.ds(l, 1), :]
                G[f, g, j, 72:73, :] = GRr[1, f, j, pl.ds(l, 1), :]
        RB = 16
        lane = lane_iota(RB)
        for b in range(64 // RB):
            r0 = 8 + RB * b
            rows = slice(r0, r0 + RB)
            out = slice(RB * b, RB * b + RB)
            sums, advs, mids = {}, {}, {}
            vels = [[V[d, l, out, 128 * j : 128 * j + 128] for j in range(2)] for d in range(3)]
            for f in range(2):
                i = f * GL + l
                mid = [G[f, g, j, rows, :] for j in range(2)]
                lo = [pltpu.roll(GCr[0, out, :], lax.rem(128 - i, 128), 1)] + [pltpu.roll(m, 1, 1) for m in mid]
                hi = [pltpu.roll(m, 127, 1) for m in mid] + [pltpu.roll(GCr[1, out, :], 127 - i, 1)]
                for j in range(2):
                    y_lo = jnp.where(lane == 0, lo[j], lo[j + 1])
                    y_hi = jnp.where(lane == 127, hi[j + 1], hi[j])
                    x_lo = G[f, g, j, r0 - 1 : r0 - 1 + RB, :]
                    x_hi = G[f, g, j, r0 + 1 : r0 + 1 + RB, :]
                    z_lo = G[f, g - 1, j, rows, :]
                    z_hi = G[f, g + 1, j, rows, :]
                    sums[f, j] = ((z_lo + z_hi) + (x_lo + x_hi)) + (y_lo + y_hi)
                    advs[f, j] = 0.5 * (
                        vels[0][j] * (z_hi - z_lo) + vels[1][j] * (x_hi - x_lo) + vels[2][j] * (y_hi - y_lo)
                    )
                    mids[f, j] = mid[j]
            for j in range(2):
                temp, fuel = mids[0, j], mids[1, j]
                reaction = fuel * jnp.exp(-4.0 / temp)
                lanes = slice(128 * j, 128 * j + 128)
                gas_out[l, out, lanes] = temp + 0.2 * (
                    0.2 * (sums[0, j] - 6.0 * temp) - advs[0, j] + 3.0 * reaction
                )
                fuel_out[l, out, lanes] = fuel + 0.2 * (
                    0.15 * (sums[1, j] - 6.0 * fuel) - advs[1, j] - reaction
                )

    def gas_layers(first, last):
        def body(l, carry):
            gas_layer(l)
            return carry

        lax.fori_loop(first, last, body, 0)

    def wall_layer(s, c, i, PL, PR, cl, cr, flux):
        l = CL * c + i
        src, dst = S.at[s % 2], S.at[(s + 1) % 2]
        lm = l - 1 if not flux else l
        for j in range(4):
            src[l, j, 7:8, :] = WRr[s, 0, j, pl.ds(l, 1), :]
            src[l, j, 40:41, :] = WRr[s, 1, j, pl.ds(l, 1), :]
        mid = [src[l, j, 8:40, :] for j in range(4)]
        lo = [pltpu.roll(PL, lax.rem(128 - i, 128), 1)] + [pltpu.roll(m, 1, 1) for m in mid]
        hi = [pltpu.roll(m, 127, 1) for m in mid] + [pltpu.roll(PR, 127 - i, 1)]
        for j in range(4):
            y_lo = jnp.where(lane32 == 0, lo[j], lo[j + 1])
            y_hi = jnp.where(lane32 == 127, hi[j + 1], hi[j])
            near = (src[lm, j, 8:40, :] + src[l + 1, j, 8:40, :]) + (src[l, j, 7:39, :] + src[l, j, 9:41, :])
            near = near + (y_lo + y_hi)
            lanes = slice(128 * j, 128 * j + 128)
            new = mid[j] + D[l, :, lanes] * (near - 6.0 * mid[j])
            if flux:
                new = new + FX[j]
            if s == STEPS - 1:
                solid_out[l, :, lanes] = new
                if flux:
                    T0[j] = new
            else:
                dst[l, j, 8:40, :] = new
                WRs[s + 1, 0, j, pl.ds(l, 1), :] = new[0:1, :]
                WRs[s + 1, 1, j, pl.ds(l, 1), :] = new[31:32, :]
                if j == 0:
                    cl = jnp.where(lane32 == i, pltpu.roll(new, i, 1), cl)
                if j == 3:
                    cr = jnp.where(lane32 == i, pltpu.roll(new, i + 1, 1), cr)
        return cl, cr

    def wall_chunk(s, c):
        for copy in wall_copies(s, c):
            copy.wait_recv()
        PL, PR = WCr[s, 0, c], WCr[s, 1, c]
        cl = cr = jnp.zeros((32, 128), F32)
        first = 0
        if c == 0:
            cl, cr = wall_layer(s, c, I32(0), PL, PR, cl, cr, True)
            first = 1

        def body(i, carry):
            return wall_layer(s, c, i, PL, PR, *carry, False)

        cl, cr = lax.fori_loop(first, CL, body, (cl, cr))
        if s < STEPS - 1:
            WCs[s + 1, 0, c] = cl
            WCs[s + 1, 1, c] = cr
            for copy in wall_copies(s + 1, c):
                copy.start()

    def wall_flux():
        for piece, (dev, self_) in enumerate(sources):
            for part in PARTS:
                copy = face_copy(0, dev, piece, part, 0)
                here = self_
                if part == 0:
                    here = self_ & (gy > 0)
                if part == 2:
                    here = self_ & (gy < 3)
                pl.when(jnp.logical_not(here))(copy.wait_recv)
        tiles = [jnp.where(FB[1, j] > 0.5, FB[0, j], -FB[0, j]) for j in range(4)]
        prow = lax.broadcasted_iota(I32, (32, 128), 0)
        half = row * 16 + lax.shift_right_logical(prow, 1)
        for k in range(4):
            if k % 2 == 0:
                a, b, shift, cut = k // 2, k // 2 + 1, 32, 32
            else:
                a, b, shift, cut = k // 2 + 1, k // 2 + 2, 96, 96
            a, b = ((0, 1), (1, 2), (1, 2), (2, 3))[k]
            window = jnp.where(lane32 < cut, pltpu.roll(tiles[a], shift, 1), pltpu.roll(tiles[b], shift, 1))
            U[pl.ds(0, 32, stride=2), :] = window
            U[pl.ds(1, 32, stride=2), :] = window
            own = OW[:, 128 * k : 128 * k + 128]
            arow = lax.shift_right_logical(own, 10)
            acol = lax.bitwise_and(own, 1023)
            shift_row = lax.bitwise_and(arow - half + DISP, 511)
            col = lax.bitwise_and(acol - (gz * 256 - 128), 1023) - (96 + 64 * k)
            value = jnp.zeros((32, 128), F32)
            for d in range(2 * DISP + 1):
                base = 16 + 2 * (d - DISP)
                picked = jnp.take_along_axis(U[base : base + 32, :], col, axis=1, mode="promise_in_bounds")
                value = jnp.where(shift_row == d, picked, value)
            gas_at = jnp.abs(value)
            film = jnp.where(value > 0.0, 0.15 * jnp.exp(0.7 * jnp.log(gas_at)), 0.0)
            FX[k] = 0.25 * (film * (gas_at - S[0, 0, k, 8:40, :]))

    loads["d"].wait()
    loads["ow"].wait()
    for c in (3, 2, 1):
        wall_chunk(0, c)
    wall_flux()
    wall_chunk(0, 0)
    loads["v"].wait()
    for copy in g_copies:
        copy.wait_recv()
    pl.when(jnp.logical_not(at_top))(z_down.wait_recv)

    @pl.when(at_top)
    def _():
        for f in range(2):
            for j in range(2):
                G[f, GL + 1, j, 8:72, :] = G[f, GL, j, 8:72, :]

    gas_layers(1, 9)
    for c in (3, 2, 1, 0):
        wall_chunk(1, c)
    gas_layers(9, 17)
    for c in (3, 2, 1, 0):
        wall_chunk(2, c)
    gas_layers(17, 25)
    for c in (0, 1, 2, 3):
        wall_chunk(3, c)

    lane16 = lane_iota(16)
    idx = lax.bitwise_and(2 * lane16, 127)
    for k in range(2):
        halves = []
        for j in (2 * k, 2 * k + 1):
            y = T0[j, pl.ds(0, 16, stride=2), :] + T0[j, pl.ds(1, 16, stride=2), :]
            y = 0.25 * (y + pltpu.roll(y, 127, 1))
            halves.append(jnp.take_along_axis(y, idx, axis=1, mode="promise_in_bounds"))
        WTs[k] = jnp.where(lane16 < 64, halves[0], halves[1])
    wt_self = (gz == 0) & (gy == 0)
    wt_rows = pl.ds(pl.multiple_of(gy * 16, 16), 16)
    wt_copy = send(WTs, WTr.at[:, wt_rows, :], t_send, t_recv.at[gy], (gx, gz, 0))
    pl.when(jnp.logical_not(wt_self))(wt_copy.start)

    @pl.when(wt_self)
    def _():
        WTr[:, 0:16, :] = WTs[...]

    gas_layers(25, GL)

    @pl.when(jnp.logical_not(at_wall))
    def _():
        z_up.wait_recv()

    @pl.when(at_wall)
    def _():
        for t in range(4):
            copy = send(WTs, WTr.at[:, pl.ds(16 * t, 16), :], t_send, t_recv.at[t], (gx, t, gy))
            here = (gy == 0) & (t == 0)
            pl.when(jnp.logical_not(here))(copy.wait_recv)
        for j in range(2):
            temp = G[0, 1, j, 8:72, :]
            G[0, 0, j, 8:72, :] = jnp.where(FS[1, j] > 0.5, 2.0 * WTr[j] - temp, temp)
            G[1, 0, j, 8:72, :] = G[1, 1, j, 8:72, :]

    gas_layers(0, 1)

    for s in range(STEPS):
        for c in range(CHUNKS):
            for copy in wall_copies(s, c):
                copy.wait_send()
    for copy in g_copies:
        copy.wait_send()
    pl.when(jnp.logical_not(at_wall))(z_down.wait_send)
    pl.when(jnp.logical_not(at_top))(z_up.wait_send)
    pl.when(jnp.logical_not(wt_self))(wt_copy.wait_send)

    @pl.when(at_wall)
    def _():
        for n, (dev, piece, part, r, self_) in enumerate(face_targets()):
            copy = face_copy(n, dev, piece, part, r)
            if self_ is None:
                copy.wait_send()
            else:
                pl.when(jnp.logical_not(self_))(copy.wait_send)


def shards(gas_temp, fuel_frac, velocity, wall_flags, solid_temp, diffusivity, gas_owner):
    hbm = pl.BlockSpec(memory_space=pltpu.HBM)
    vmem = pl.BlockSpec(memory_space=pltpu.VMEM)
    gas_shape, solid_shape = gas_temp.shape, solid_temp.shape
    dma = pltpu.SemaphoreType.DMA
    buf = pltpu.VMEM
    results = [gas_shape, gas_shape, solid_shape]
    return pl.pallas_call(
        kernel,
        out_shape=[pltpu.VMEM(s, F32) for s in results],
        in_specs=[hbm] * 7,
        out_specs=[vmem] * 3,
        scratch_shapes=[
            buf((2, GL + 2, 2, 80, 128), F32),
            buf((3, GL, 64, 256), F32),
            buf((2, NL + 1, 4, 48, 128), F32),
            buf((NL, 32, 512), F32),
            buf((64, 256), I32),
            buf((32, 512), I32),
            buf((2, 2, 64, 128), F32),
            buf((2, 4, 32, 128), F32),
            buf((64, 128), F32),
            buf((4, 32, 128), F32),
            buf((STEPS, 2, 4, NL, 128), F32),
            buf((STEPS, 2, 4, NL, 128), F32),
            buf((STEPS, 2, CHUNKS, 32, 128), F32),
            buf((STEPS, 2, CHUNKS, 32, 128), F32),
            buf((2, 2, 2, GL, 128), F32),
            buf((2, 2, 2, GL, 128), F32),
            buf((2, 64, 128), F32),
            buf((2, 64, 128), F32),
            buf((4, 32, 128), F32),
            buf((2, 16, 128), F32),
            buf((2, 64, 128), F32),
            dma((12,)),
            dma((STEPS, CHUNKS, 4)),
            dma((STEPS, CHUNKS, 4)),
            dma((6,)),
            dma((6,)),
            dma((36,)),
            dma((3, 3)),
            dma,
            dma((4,)),
        ],
        compiler_params=pltpu.CompilerParams(
            collective_id=0, has_side_effects=True, vmem_limit_bytes=52 * 1024 * 1024
        ),
        name="section",
    )(gas_temp, fuel_frac, velocity, wall_flags, solid_temp, diffusivity, gas_owner)


def solution(mesh):
    placed = (
        P("gz", "gx", "gy"),
        P("gz", "gx", "gy"),
        P(None, "gz", "gx", "gy"),
        P("gx", "gy"),
        P(None, ("gx", "gy"), "gz"),
        P(None, ("gx", "gy"), "gz"),
        P(("gx", "gy"), "gz"),
    )
    return jax.shard_map(
        shards,
        mesh=mesh,
        in_specs=placed,
        out_specs=(P("gz", "gx", "gy"), P("gz", "gx", "gy"), P(None, ("gx", "gy"), "gz")),
        check_vma=False,
    )
```

profile of v0, /device:TPU:1, one launch (start us, length us, event | category | flops | bytes accessed | tf_op | source)
XLA Modules:
  0.0 82.3 jit_solution(18208633303159893678)
XLA Ops:
  0.6 77.0 %section.1 = (f32[32,64,256]{2,1,0:T(8,128)S(1)}, f32[32,64,256]{2,1,0:T(8,128)S(1)}, f32[64,32,512]{2,1,0:T(8,128)S(1)}) custom-call(f32[32,64,256]{2,1,0:T(8,128)} %gas_ref.1, f32[32,64,256]{2,1,0:T(8,128)} %fuel_ref.1, f32[3,32,64,256]{3,2,1,0:T(8,128)} %vel_ref.1, s32[64,256]{1,0:T(8,128)} %flags_ref.1, f32[64,32,512]{2,1,0:T(8,128)} %solid_ref.1, ...), custom_call_target="tpu_custom_call" | custom-call | tf_op jit(solution)/shard_map/section/pallas_call | solution.py:499
  77.7 1.3 %copy.13 = f32[32,64,256]{2,1,0:T(8,128)} copy(f32[32,64,256]{2,1,0:T(8,128)S(1)} %get-tuple-element.3) | data formatting | bytes 4194304
  79.0 1.3 %copy.14 = f32[32,64,256]{2,1,0:T(8,128)} copy(f32[32,64,256]{2,1,0:T(8,128)S(1)} %get-tuple-element.4) | data formatting | bytes 4194304
  80.3 2.0 %copy.15 = f32[64,32,512]{2,1,0:T(8,128)} copy(f32[64,32,512]{2,1,0:T(8,128)S(1)} %get-tuple-element.5) | data formatting | bytes 8388608
where the time goes:
time: 83.1 us; the launch traced here: 82.3 us
  Pallas kernels  77 us (93%)
  local copies, waits for them, and re-layouts  4.65 us (6%)
    pallas_call x1, Pallas kernels, shards(): pl.pallas_call(kernel, out_shape=[pltpu.VMEM(s, F32) for s in results], i...  77 us
    unnamed x3, local copies, waits for them, and re-layouts  4.65 us

commit v1 on v0

--- a/solution.py
+++ b/solution.py
@@ -15,6 +15,10 @@
 CHUNKS = 4
 CL = 16
 NL = 64
+WU = 4
+PU = 4
+GAS_1 = 13
+GAS_2 = 21
 GL = 32
 DISP = 4
 
@@ -36,7 +40,7 @@
     gas_ref, fuel_ref, vel_ref, flags_ref, solid_ref, diff_ref, owner_ref,
     gas_out, fuel_out, solid_out,
     G, V, S, D, FL, OW, FS, FB, U, FX,
-    WRs, WRr, WCs, WCr, GRs, GRr, GCs, GCr, T0, WTs, WTr,
+    WRs, WRr, WCs, WCr, WC, GRs, GRr, GCs, GCr, GC, T0, WTs, WTr,
     lsem, w_send, w_recv, g_send, g_recv, f_send, f_recv, t_send, t_recv,
 ):
     gx, gy, gz = lax.axis_index("gx"), lax.axis_index("gy"), lax.axis_index("gz")
@@ -155,12 +159,12 @@
         )
 
     def wall_copies(s, c):
-        rows = pl.ds(CL * c, CL)
+        rows = pl.ds(c * CL if isinstance(c, int) else pl.multiple_of(c * CL, CL), CL)
         return (
             send(WRs.at[s, 0, :, rows, :], WRr.at[s, 1, :, rows, :], w_send.at[s, c, 0], w_recv.at[s, c, 1], up_dev),
             send(WRs.at[s, 1, :, rows, :], WRr.at[s, 0, :, rows, :], w_send.at[s, c, 1], w_recv.at[s, c, 0], down_dev),
-            send(WCs.at[s, 0, c], WCr.at[s, 1, c], w_send.at[s, c, 2], w_recv.at[s, c, 3], left_dev),
-            send(WCs.at[s, 1, c], WCr.at[s, 0, c], w_send.at[s, c, 3], w_recv.at[s, c, 2], right_dev),
+            send(WCs.at[s, c], WCr.at[s, 1, c], w_send.at[s, c, 2], w_recv.at[s, c, 3], left_dev),
+            send(WCs.at[s, c], WCr.at[s, 0, c], w_send.at[s, c, 3], w_recv.at[s, c, 2], right_dev),
         )
 
     lane32 = lane_iota(32)
@@ -169,21 +173,27 @@
     for j in range(4):
         loads["s", j].wait()
 
-    for c in range(CHUNKS):
-        def pack(i, carry, c=c):
-            cl, cr = carry
-            l = CL * c + i
-            for j in range(4):
-                WRs[0, 0, j, pl.ds(l, 1), :] = S[0, l, j, 8:9, :]
-                WRs[0, 1, j, pl.ds(l, 1), :] = S[0, l, j, 39:40, :]
-            cl = jnp.where(lane32 == i, pltpu.roll(S[0, l, 0, 8:40, :], i, 1), cl)
-            cr = jnp.where(lane32 == i, pltpu.roll(S[0, l, 3, 8:40, :], i + 1, 1), cr)
-            return cl, cr
-
-        zero = jnp.zeros((32, 128), F32)
-        cl, cr = lax.fori_loop(0, CL, pack, (zero, zero))
-        WCs[0, 0, c] = cl
-        WCs[0, 1, c] = cr
+    zero32 = jnp.zeros((32, 128), F32)
+
+    def columns(acc, first, last, i, lane):
+        both = pltpu.roll(jnp.where(lane < 64, first, last), 2 * i + 1, 1)
+        return jnp.where(lax.shift_right_arithmetic(lane, 1) == i, both, acc)
+
+    def pack_chunk(c, carry):
+        def pack(n, acc):
+            for k in range(PU):
+                i = PU * n + k
+                l = CL * c + i
+                for j in range(4):
+                    WRs[0, 0, j, pl.ds(l, 1), :] = S[0, l, j, 8:9, :]
+                    WRs[0, 1, j, pl.ds(l, 1), :] = S[0, l, j, 39:40, :]
+                acc = columns(acc, S[0, l, 0, 8:40, :], S[0, l, 3, 8:40, :], i, lane32)
+            return acc
+
+        WCs[0, c] = lax.fori_loop(0, CL // PU, pack, zero32)
+        return carry
+
+    lax.fori_loop(0, CHUNKS, pack_chunk, 0)
 
     for key in (("g0", 0), ("g0", 1), "fl", ("g1", 0), ("g1", 1)):
         loads[key].wait()
@@ -191,27 +201,19 @@
         FS[0, j] = G[0, 1, j, 8:72, :]
         FS[1, j] = FL[:, 128 * j : 128 * j + 128].astype(F32)
 
-    def gpack(l, carry):
-        cl, cr = carry
-        for f in range(2):
-            for j in range(2):
-                GRs[0, f, j, pl.ds(l, 1), :] = G[f, l + 1, j, 8:9, :]
-                GRs[1, f, j, pl.ds(l, 1), :] = G[f, l + 1, j, 71:72, :]
-            i = f * GL + l
-            cl = jnp.where(lane64 == i, pltpu.roll(G[f, l + 1, 0, 8:72, :], i, 1), cl)
-            cr = jnp.where(lane64 == i, pltpu.roll(G[f, l + 1, 1, 8:72, :], i + 1, 1), cr)
-        return cl, cr
-
-    zero = jnp.zeros((64, 128), F32)
-    cl, cr = lax.fori_loop(0, GL, gpack, (zero, zero))
-    GCs[0] = cl
-    GCs[1] = cr
+    def gpack(n, acc):
+        for k in range(2):
+            l = 2 * n + k
+            for f in range(2):
+                for j in range(2):
+                    GRs[0, f, j, pl.ds(l, 1), :] = G[f, l + 1, j, 8:9, :]
+                    GRs[1, f, j, pl.ds(l, 1), :] = G[f, l + 1, j, 71:72, :]
+                acc = columns(acc, G[f, l + 1, 0, 8:72, :], G[f, l + 1, 1, 8:72, :], f * GL + l, lane64)
+        return acc
+
+    GCs[...] = lax.fori_loop(0, GL // 2, gpack, jnp.zeros((64, 128), F32))
 
     pl.semaphore_wait(barrier, count)
-
-    for c in reversed(range(CHUNKS)):
-        for copy in wall_copies(0, c):
-            copy.start()
 
     def face_ref(buf, piece):
         return buf.at[:, pl.ds(1, 2)] if piece == 0 else buf.at[:, pl.ds(0 if piece == 1 else 3, 1)]
@@ -240,6 +242,18 @@
         else:
             FB[:, 3, start : start + size, :] = FS[:, 0, r : r + size, :]
 
+    g_copies = (
+        send(GRs.at[0], GRr.at[1], g_send.at[0], g_recv.at[1], gxm_dev),
+        send(GRs.at[1], GRr.at[0], g_send.at[1], g_recv.at[0], gxp_dev),
+        send(GCs, GCr.at[1], g_send.at[2], g_recv.at[3], gym_dev),
+        send(GCs, GCr.at[0], g_send.at[3], g_recv.at[2], gyp_dev),
+    )
+    for copy in g_copies:
+        copy.start()
+    for c in reversed(range(CHUNKS)):
+        for copy in wall_copies(0, c):
+            copy.start()
+
     @pl.when(at_wall)
     def _():
         for n, (dev, piece, part, r, self_) in enumerate(face_targets()):
@@ -250,14 +264,6 @@
                 pl.when(jnp.logical_not(self_))(copy.start)
                 pl.when(self_)(functools.partial(face_here, piece, part, r))
 
-    g_copies = (
-        send(GRs.at[0], GRr.at[1], g_send.at[0], g_recv.at[1], gxm_dev),
-        send(GRs.at[1], GRr.at[0], g_send.at[1], g_recv.at[0], gxp_dev),
-        send(GCs.at[0], GCr.at[1], g_send.at[2], g_recv.at[3], gym_dev),
-        send(GCs.at[1], GCr.at[0], g_send.at[3], g_recv.at[2], gyp_dev),
-    )
-    for copy in g_copies:
-        copy.start()
     z_down = send(
         G.at[:, 1, :, pl.ds(8, 64), :], G.at[:, GL + 1, :, pl.ds(8, 64), :], g_send.at[4], g_recv.at[5], left_dev
     )
@@ -284,8 +290,9 @@
             for f in range(2):
                 i = f * GL + l
                 mid = [G[f, g, j, rows, :] for j in range(2)]
-                lo = [pltpu.roll(GCr[0, out, :], lax.rem(128 - i, 128), 1)] + [pltpu.roll(m, 1, 1) for m in mid]
-                hi = [pltpu.roll(m, 127, 1) for m in mid] + [pltpu.roll(GCr[1, out, :], 127 - i, 1)]
+                edge = pltpu.roll(GC[out, :], lax.bitwise_and(128 - 2 * i, 127), 1)
+                lo = [edge] + [pltpu.roll(m, 1, 1) for m in mid]
+                hi = [pltpu.roll(m, 127, 1) for m in mid] + [edge]
                 for j in range(2):
                     y_lo = jnp.where(lane == 0, lo[j], lo[j + 1])
                     y_hi = jnp.where(lane == 127, hi[j + 1], hi[j])
@@ -316,58 +323,70 @@
 
         lax.fori_loop(first, last, body, 0)
 
-    def wall_layer(s, c, i, PL, PR, cl, cr, flux):
-        l = CL * c + i
+    def wall_pack(s, c, g, acc):
+        dst = S.at[(s + 1) % 2]
+        for k in range(WU):
+            i = WU * g + k
+            l = jnp.maximum(CL * c + i, 0)
+            acc = columns(acc, dst[l, 0, 8:40, :], dst[l, 3, 8:40, :], i, lane32)
+        return acc
+
+    def wall_group(s, c, g, acc):
         src, dst = S.at[s % 2], S.at[(s + 1) % 2]
-        lm = l - 1 if not flux else l
-        for j in range(4):
-            src[l, j, 7:8, :] = WRr[s, 0, j, pl.ds(l, 1), :]
-            src[l, j, 40:41, :] = WRr[s, 1, j, pl.ds(l, 1), :]
-        mid = [src[l, j, 8:40, :] for j in range(4)]
-        lo = [pltpu.roll(PL, lax.rem(128 - i, 128), 1)] + [pltpu.roll(m, 1, 1) for m in mid]
-        hi = [pltpu.roll(m, 127, 1) for m in mid] + [pltpu.roll(PR, 127 - i, 1)]
-        for j in range(4):
-            y_lo = jnp.where(lane32 == 0, lo[j], lo[j + 1])
-            y_hi = jnp.where(lane32 == 127, hi[j + 1], hi[j])
-            near = (src[lm, j, 8:40, :] + src[l + 1, j, 8:40, :]) + (src[l, j, 7:39, :] + src[l, j, 9:41, :])
-            near = near + (y_lo + y_hi)
-            lanes = slice(128 * j, 128 * j + 128)
-            new = mid[j] + D[l, :, lanes] * (near - 6.0 * mid[j])
-            if flux:
-                new = new + FX[j]
-            if s == STEPS - 1:
-                solid_out[l, :, lanes] = new
-                if flux:
-                    T0[j] = new
-            else:
-                dst[l, j, 8:40, :] = new
-                WRs[s + 1, 0, j, pl.ds(l, 1), :] = new[0:1, :]
-                WRs[s + 1, 1, j, pl.ds(l, 1), :] = new[31:32, :]
-                if j == 0:
-                    cl = jnp.where(lane32 == i, pltpu.roll(new, i, 1), cl)
-                if j == 3:
-                    cr = jnp.where(lane32 == i, pltpu.roll(new, i + 1, 1), cr)
-        return cl, cr
+        if s < STEPS - 1:
+            acc = wall_pack(s, c, g - 1, acc)
+        for k in range(WU):
+            i = WU * g + k
+            l = CL * c + i
+            for j in range(4):
+                src[l, j, 7:8, :] = WRr[s, 0, j, pl.ds(l, 1), :]
+                src[l, j, 40:41, :] = WRr[s, 1, j, pl.ds(l, 1), :]
+        for k in range(WU):
+            i = WU * g + k
+            l = CL * c + i
+            lm = jnp.maximum(l - 1, 0) if k == 0 else l - 1
+            mid = [src[l, j, 8:40, :] for j in range(4)]
+            edge = pltpu.roll(WC[...], lax.bitwise_and(128 - 2 * i, 127), 1)
+            lo = [edge] + [pltpu.roll(m, 1, 1) for m in mid]
+            hi = [pltpu.roll(m, 127, 1) for m in mid] + [edge]
+            for j in range(4):
+                y_lo = jnp.where(lane32 == 0, lo[j], lo[j + 1])
+                y_hi = jnp.where(lane32 == 127, hi[j + 1], hi[j])
+                near = (src[lm, j, 8:40, :] + src[l + 1, j, 8:40, :]) + (src[l, j, 7:39, :] + src[l, j, 9:41, :])
+                near = near + (y_lo + y_hi)
+                lanes = slice(128 * j, 128 * j + 128)
+                new = mid[j] + D[l, :, lanes] * (near - 6.0 * mid[j])
+                if k == 0:
+                    new = new + jnp.where(l == 0, FX[j], 0.0)
+                if s == STEPS - 1:
+                    solid_out[l, :, lanes] = new
+                else:
+                    dst[l, j, 8:40, :] = new
+                    WRs[s + 1, 0, j, pl.ds(l, 1), :] = new[0:1, :]
+                    WRs[s + 1, 1, j, pl.ds(l, 1), :] = new[31:32, :]
+        return acc
 
     def wall_chunk(s, c):
         for copy in wall_copies(s, c):
             copy.wait_recv()
-        PL, PR = WCr[s, 0, c], WCr[s, 1, c]
-        cl = cr = jnp.zeros((32, 128), F32)
-        first = 0
-        if c == 0:
-            cl, cr = wall_layer(s, c, I32(0), PL, PR, cl, cr, True)
-            first = 1
-
-        def body(i, carry):
-            return wall_layer(s, c, i, PL, PR, *carry, False)
-
-        cl, cr = lax.fori_loop(first, CL, body, (cl, cr))
+        even = lax.bitwise_and(lane32, 1) == 0
+        WC[...] = jnp.where(even, WCr[s, 0, c], pltpu.roll(WCr[s, 1, c], 126, 1))
+
+        def body(g, acc):
+            return wall_group(s, c, g, acc)
+
+        acc = lax.fori_loop(0, CL // WU, body, zero32)
         if s < STEPS - 1:
-            WCs[s + 1, 0, c] = cl
-            WCs[s + 1, 1, c] = cr
+            WCs[s + 1, c] = wall_pack(s, c, CL // WU - 1, acc)
             for copy in wall_copies(s + 1, c):
                 copy.start()
+
+    def wall_step(s, first, last, down):
+        def body(n, carry):
+            wall_chunk(s, CHUNKS - 1 - n if down else n)
+            return carry
+
+        lax.fori_loop(first, last, body, 0)
 
     def wall_flux():
         for piece, (dev, self_) in enumerate(sources):
@@ -405,32 +424,21 @@
             film = jnp.where(value > 0.0, 0.15 * jnp.exp(0.7 * jnp.log(gas_at)), 0.0)
             FX[k] = 0.25 * (film * (gas_at - S[0, 0, k, 8:40, :]))
 
-    loads["d"].wait()
-    loads["ow"].wait()
-    for c in (3, 2, 1):
-        wall_chunk(0, c)
-    wall_flux()
-    wall_chunk(0, 0)
     loads["v"].wait()
     for copy in g_copies:
         copy.wait_recv()
-    pl.when(jnp.logical_not(at_top))(z_down.wait_recv)
-
-    @pl.when(at_top)
-    def _():
-        for f in range(2):
-            for j in range(2):
-                G[f, GL + 1, j, 8:72, :] = G[f, GL, j, 8:72, :]
-
-    gas_layers(1, 9)
-    for c in (3, 2, 1, 0):
-        wall_chunk(1, c)
-    gas_layers(9, 17)
-    for c in (3, 2, 1, 0):
-        wall_chunk(2, c)
-    gas_layers(17, 25)
-    for c in (0, 1, 2, 3):
-        wall_chunk(3, c)
+    GC[...] = jnp.where(lax.bitwise_and(lane64, 1) == 0, GCr[0], pltpu.roll(GCr[1], 126, 1))
+    gas_layers(1, GAS_1)
+    loads["d"].wait()
+    loads["ow"].wait()
+    wall_flux()
+    wall_step(0, 0, CHUNKS, True)
+    wall_step(1, 0, CHUNKS, True)
+    gas_layers(GAS_1, GAS_2)
+    wall_step(2, 0, CHUNKS, False)
+    wall_chunk(3, 0)
+    for j in range(4):
+        T0[j] = solid_out[0, :, 128 * j : 128 * j + 128]
 
     lane16 = lane_iota(16)
     idx = lax.bitwise_and(2 * lane16, 127)
@@ -450,7 +458,17 @@
     def _():
         WTr[:, 0:16, :] = WTs[...]
 
-    gas_layers(25, GL)
+    wall_step(3, 1, CHUNKS, False)
+    gas_layers(GAS_2, GL - 1)
+    pl.when(jnp.logical_not(at_top))(z_down.wait_recv)
+
+    @pl.when(at_top)
+    def _():
+        for f in range(2):
+            for j in range(2):
+                G[f, GL + 1, j, 8:72, :] = G[f, GL, j, 8:72, :]
+
+    gas_layers(GL - 1, GL)
 
     @pl.when(jnp.logical_not(at_wall))
     def _():
@@ -514,12 +532,14 @@
             buf((4, 32, 128), F32),
             buf((STEPS, 2, 4, NL, 128), F32),
             buf((STEPS, 2, 4, NL, 128), F32),
+            buf((STEPS, CHUNKS, 32, 128), F32),
             buf((STEPS, 2, CHUNKS, 32, 128), F32),
-            buf((STEPS, 2, CHUNKS, 32, 128), F32),
+            buf((32, 128), F32),
             buf((2, 2, 2, GL, 128), F32),
             buf((2, 2, 2, GL, 128), F32),
+            buf((64, 128), F32),
             buf((2, 64, 128), F32),
-            buf((2, 64, 128), F32),
+            buf((64, 128), F32),
             buf((4, 32, 128), F32),
             buf((2, 16, 128), F32),
             buf((2, 64, 128), F32),

time: 83.1 us -> 61 us (0.73)
  Pallas kernels: 77 us -> 55.1 us
    pallas_call x1, Pallas kernels: 77 us -> 55.1 us  [shards(): pl.pallas_call(kernel, out_shape=[pltpu.VMEM(s, F32) for s in results], i...]
where the time goes in v1:
time: 61 us; the launch traced here: 60.4 us
  Pallas kernels  55.1 us (90%)
  local copies, waits for them, and re-layouts  4.65 us (8%)
  between operations  0.64 us (1%)
    pallas_call x1, Pallas kernels, shards(): pl.pallas_call(kernel, out_shape=[pltpu.VMEM(s, F32) for s in results], i...  55.1 us
    unnamed x3, local copies, waits for them, and re-layouts  4.65 us

profile of v1, /device:TPU:1, one launch (start us, length us, event | category | flops | bytes accessed | tf_op | source)
XLA Modules:
  0.0 60.4 jit_solution(17359130358972108198)
XLA Ops:
  0.6 55.1 %section.1 = (f32[32,64,256]{2,1,0:T(8,128)S(1)}, f32[32,64,256]{2,1,0:T(8,128)S(1)}, f32[64,32,512]{2,1,0:T(8,128)S(1)}) custom-call(f32[32,64,256]{2,1,0:T(8,128)} %gas_ref.1, f32[32,64,256]{2,1,0:T(8,128)} %fuel_ref.1, f32[3,32,64,256]{3,2,1,0:T(8,128)} %vel_ref.1, s32[64,256]{1,0:T(8,128)} %flags_ref.1, f32[64,32,512]{2,1,0:T(8,128)} %solid_ref.1, ...), custom_call_target="tpu_custom_call" | custom-call | tf_op jit(solution)/shard_map/section/pallas_call | solution.py:517
  55.8 1.3 %copy.13 = f32[32,64,256]{2,1,0:T(8,128)} copy(f32[32,64,256]{2,1,0:T(8,128)S(1)} %get-tuple-element.3) | data formatting | bytes 4194304
  57.1 1.3 %copy.14 = f32[32,64,256]{2,1,0:T(8,128)} copy(f32[32,64,256]{2,1,0:T(8,128)S(1)} %get-tuple-element.4) | data formatting | bytes 4194304
  58.4 2.0 %copy.15 = f32[64,32,512]{2,1,0:T(8,128)} copy(f32[64,32,512]{2,1,0:T(8,128)S(1)} %get-tuple-element.5) | data formatting | bytes 8388608

commit v2 on v1

--- a/solution.py
+++ b/solution.py
@@ -17,8 +17,7 @@
 NL = 64
 WU = 4
 PU = 4
-GAS_1 = 13
-GAS_2 = 21
+GAS = (12, 18, 24, 30)
 GL = 32
 DISP = 4
 
@@ -63,6 +62,11 @@
 
     loads = {}
     n = 0
+    for j in range(4):
+        loads["s", j] = local(
+            solid_ref.at[:, :, pl.ds(128 * j, 128)], S.at[0, pl.ds(0, NL), j, pl.ds(8, 32), :], lsem.at[n]
+        )
+        n += 1
     for j in range(2):
         loads["g0", j] = local(
             gas_ref.at[:, :, pl.ds(128 * j, 128)], G.at[0, pl.ds(1, GL), j, pl.ds(8, 64), :], lsem.at[n]
@@ -70,11 +74,6 @@
         n += 1
     loads["fl"] = local(flags_ref, FL, lsem.at[n])
     n += 1
-    for j in range(4):
-        loads["s", j] = local(
-            solid_ref.at[:, :, pl.ds(128 * j, 128)], S.at[0, pl.ds(0, NL), j, pl.ds(8, 32), :], lsem.at[n]
-        )
-        n += 1
     for j in range(2):
         loads["g1", j] = local(
             fuel_ref.at[:, :, pl.ds(128 * j, 128)], G.at[1, pl.ds(1, GL), j, pl.ds(8, 64), :], lsem.at[n]
@@ -161,10 +160,10 @@
     def wall_copies(s, c):
         rows = pl.ds(c * CL if isinstance(c, int) else pl.multiple_of(c * CL, CL), CL)
         return (
-            send(WRs.at[s, 0, :, rows, :], WRr.at[s, 1, :, rows, :], w_send.at[s, c, 0], w_recv.at[s, c, 1], up_dev),
-            send(WRs.at[s, 1, :, rows, :], WRr.at[s, 0, :, rows, :], w_send.at[s, c, 1], w_recv.at[s, c, 0], down_dev),
-            send(WCs.at[s, c], WCr.at[s, 1, c], w_send.at[s, c, 2], w_recv.at[s, c, 3], left_dev),
-            send(WCs.at[s, c], WCr.at[s, 0, c], w_send.at[s, c, 3], w_recv.at[s, c, 2], right_dev),
+            send(WRs.at[s, 0, :, rows, :], WRr.at[s, 1, :, rows, :], w_send.at[0], w_recv.at[s, c, 1], up_dev),
+            send(WRs.at[s, 1, :, rows, :], WRr.at[s, 0, :, rows, :], w_send.at[1], w_recv.at[s, c, 0], down_dev),
+            send(WCs.at[s, c], WCr.at[s, 1, c], w_send.at[2], w_recv.at[s, c, 3], left_dev),
+            send(WCs.at[s, c], WCr.at[s, 0, c], w_send.at[3], w_recv.at[s, c, 2], right_dev),
         )
 
     lane32 = lane_iota(32)
@@ -250,7 +249,7 @@
     )
     for copy in g_copies:
         copy.start()
-    for c in reversed(range(CHUNKS)):
+    for c in range(CHUNKS):
         for copy in wall_copies(0, c):
             copy.start()
 
@@ -428,14 +427,16 @@
     for copy in g_copies:
         copy.wait_recv()
     GC[...] = jnp.where(lax.bitwise_and(lane64, 1) == 0, GCr[0], pltpu.roll(GCr[1], 126, 1))
-    gas_layers(1, GAS_1)
+    gas_layers(1, GAS[0])
     loads["d"].wait()
     loads["ow"].wait()
     wall_flux()
-    wall_step(0, 0, CHUNKS, True)
-    wall_step(1, 0, CHUNKS, True)
-    gas_layers(GAS_1, GAS_2)
+    wall_step(0, 0, CHUNKS, False)
+    gas_layers(GAS[0], GAS[1])
+    wall_step(1, 0, CHUNKS, False)
+    gas_layers(GAS[1], GAS[2])
     wall_step(2, 0, CHUNKS, False)
+    gas_layers(GAS[2], GAS[3])
     wall_chunk(3, 0)
     for j in range(4):
         T0[j] = solid_out[0, :, 128 * j : 128 * j + 128]
@@ -459,7 +460,7 @@
         WTr[:, 0:16, :] = WTs[...]
 
     wall_step(3, 1, CHUNKS, False)
-    gas_layers(GAS_2, GL - 1)
+    gas_layers(GAS[3], GL - 1)
     pl.when(jnp.logical_not(at_top))(z_down.wait_recv)
 
     @pl.when(at_top)
@@ -487,10 +488,10 @@
 
     gas_layers(0, 1)
 
-    for s in range(STEPS):
-        for c in range(CHUNKS):
-            for copy in wall_copies(s, c):
-                copy.wait_send()
+    send(WRs.at[:, 0], WRr.at[:, 1], w_send.at[0], w_recv.at[0, 0, 1], up_dev).wait_send()
+    send(WRs.at[:, 1], WRr.at[:, 0], w_send.at[1], w_recv.at[0, 0, 0], down_dev).wait_send()
+    send(WCs, WCr.at[:, 1], w_send.at[2], w_recv.at[0, 0, 3], left_dev).wait_send()
+    send(WCs, WCr.at[:, 0], w_send.at[3], w_recv.at[0, 0, 2], right_dev).wait_send()
     for copy in g_copies:
         copy.wait_send()
     pl.when(jnp.logical_not(at_wall))(z_down.wait_send)
@@ -507,6 +508,16 @@
                 pl.when(jnp.logical_not(self_))(copy.wait_send)
 
 
+def writer(a_ref, b_ref, c_ref, a_out, b_out, c_out, sems):
+    copies = []
+    for src, dst in ((a_ref, a_out), (b_ref, b_out), (c_ref, c_out)):
+        part = src.shape[0] // 4
+        for k in range(4):
+            copies.append(local(src.at[pl.ds(k * part, part)], dst.at[pl.ds(k * part, part)], sems.at[len(copies)]))
+    for copy in copies:
+        copy.wait()
+
+
 def shards(gas_temp, fuel_frac, velocity, wall_flags, solid_temp, diffusivity, gas_owner):
     hbm = pl.BlockSpec(memory_space=pltpu.HBM)
     vmem = pl.BlockSpec(memory_space=pltpu.VMEM)
@@ -514,7 +525,7 @@
     dma = pltpu.SemaphoreType.DMA
     buf = pltpu.VMEM
     results = [gas_shape, gas_shape, solid_shape]
-    return pl.pallas_call(
+    results_here = pl.pallas_call(
         kernel,
         out_shape=[pltpu.VMEM(s, F32) for s in results],
         in_specs=[hbm] * 7,
@@ -544,7 +555,7 @@
             buf((2, 16, 128), F32),
             buf((2, 64, 128), F32),
             dma((12,)),
-            dma((STEPS, CHUNKS, 4)),
+            dma((4,)),
             dma((STEPS, CHUNKS, 4)),
             dma((6,)),
             dma((6,)),
@@ -558,6 +569,16 @@
         ),
         name="section",
     )(gas_temp, fuel_frac, velocity, wall_flags, solid_temp, diffusivity, gas_owner)
+    results_here = [pltpu.with_memory_space_constraint(r, pltpu.VMEM) for r in results_here]
+    return pl.pallas_call(
+        writer,
+        out_shape=[jax.ShapeDtypeStruct(s, F32) for s in results],
+        in_specs=[vmem] * 3,
+        out_specs=[hbm] * 3,
+        scratch_shapes=[dma((12,))],
+        compiler_params=pltpu.CompilerParams(vmem_limit_bytes=2 * 1024 * 1024),
+        name="writer",
+    )(*results_here)
 
 
 def solution(mesh):

time: 61 us -> 54 us (0.89)
  local copies, waits for them, and re-layouts: 4.65 us -> 0 us
  Pallas kernels: 55.1 us -> 53.2 us
    pallas_call x1, Pallas kernels: 55.1 us -> 49.8 us  [shards(): pl.pallas_call(kernel, out_shape=[pltpu.VMEM(s, F32) for s in results], i...]
    unnamed x3 -> x0, local copies, waits for them, and re-layouts: 4.65 us -> none
    pallas_call x0 -> x1, Pallas kernels: none -> 3.4 us  [shards(): pl.pallas_call(writer, out_shape=[jax.ShapeDtypeStruct(s, F32) for s in r...]
where the time goes in v2:
time: 54 us; the launch traced here: 53.9 us
  Pallas kernels  53.2 us (99%)
  between operations  0.64 us (1%)
    pallas_call x1, Pallas kernels, shards(): pl.pallas_call(kernel, out_shape=[pltpu.VMEM(s, F32) for s in results], i...  49.8 us
    pallas_call x1, Pallas kernels, shards(): pl.pallas_call(writer, out_shape=[jax.ShapeDtypeStruct(s, F32) for s in r...  3.4 us

profile of v2, /device:TPU:1, one launch (start us, length us, event | category | flops | bytes accessed | tf_op | source)
XLA Modules:
  0.0 53.9 jit_solution(11297513932250605983)
XLA Ops:
  0.6 49.8 %section.1 = (f32[32,64,256]{2,1,0:T(8,128)S(1)}, f32[32,64,256]{2,1,0:T(8,128)S(1)}, f32[64,32,512]{2,1,0:T(8,128)S(1)}) custom-call(f32[32,64,256]{2,1,0:T(8,128)} %gas_ref.1, f32[32,64,256]{2,1,0:T(8,128)} %fuel_ref.1, f32[3,32,64,256]{3,2,1,0:T(8,128)} %vel_ref.1, s32[64,256]{1,0:T(8,128)} %flags_ref.1, f32[64,32,512]{2,1,0:T(8,128)} %solid_ref.1, ...), custom_call_target="tpu_custom_call" | custom-call | tf_op jit(solution)/shard_map/section/pallas_call | solution.py:528
  50.5 3.4 %writer.1 = (f32[32,64,256]{2,1,0:T(8,128)}, f32[32,64,256]{2,1,0:T(8,128)}, f32[64,32,512]{2,1,0:T(8,128)}) custom-call(f32[32,64,256]{2,1,0:T(8,128)S(1)} %get-tuple-element.6.a_ref, f32[32,64,256]{2,1,0:T(8,128)S(1)} %get-tuple-element.7.b_ref, f32[64,32,512]{2,1,0:T(8,128)S(1)} %get-tuple-element.8.c_ref), custom_call_target="tpu_custom_call" | custom-call | tf_op jit(solution)/shard_map/writer/pallas_call | solution.py:573

commit v3 on v2

--- a/solution.py
+++ b/solution.py
@@ -15,9 +15,11 @@
 CHUNKS = 4
 CL = 16
 NL = 64
-WU = 4
+HU = 2
+WU = 2 * HU
 PU = 4
-GAS = (12, 18, 24, 30)
+GAS = (1, 11, 21, 31)
+EDGES = (1, 9, 31)
 GL = 32
 DISP = 4
 
@@ -38,8 +40,8 @@
 def kernel(
     gas_ref, fuel_ref, vel_ref, flags_ref, solid_ref, diff_ref, owner_ref,
     gas_out, fuel_out, solid_out,
-    G, V, S, D, FL, OW, FS, FB, U, FX,
-    WRs, WRr, WCs, WCr, WC, GRs, GRr, GCs, GCr, GC, T0, WTs, WTr,
+    G, V, S0, S1, D, FL, OW, FS, FB, U, FX,
+    WRs, WRr, WCs, WCr, WC, RA, RB, GRs, GRr, GCs, GCr, GC, T0, WTs, WTr,
     lsem, w_send, w_recv, g_send, g_recv, f_send, f_recv, t_send, t_recv,
 ):
     gx, gy, gz = lax.axis_index("gx"), lax.axis_index("gy"), lax.axis_index("gz")
@@ -61,29 +63,25 @@
     gyp_dev = (gx, lax.rem(gy + 1, 4), gz)
 
     loads = {}
-    n = 0
     for j in range(4):
         loads["s", j] = local(
-            solid_ref.at[:, :, pl.ds(128 * j, 128)], S.at[0, pl.ds(0, NL), j, pl.ds(8, 32), :], lsem.at[n]
+            solid_ref.at[:, :, pl.ds(128 * j, 128)], S0.at[pl.ds(0, NL), j, pl.ds(8, 32), :], lsem.at[j]
         )
-        n += 1
     for j in range(2):
-        loads["g0", j] = local(
-            gas_ref.at[:, :, pl.ds(128 * j, 128)], G.at[0, pl.ds(1, GL), j, pl.ds(8, 64), :], lsem.at[n]
-        )
-        n += 1
-    loads["fl"] = local(flags_ref, FL, lsem.at[n])
-    n += 1
-    for j in range(2):
-        loads["g1", j] = local(
-            fuel_ref.at[:, :, pl.ds(128 * j, 128)], G.at[1, pl.ds(1, GL), j, pl.ds(8, 64), :], lsem.at[n]
-        )
-        n += 1
-    loads["ow"] = local(owner_ref, OW, lsem.at[n])
-    n += 1
-    loads["v"] = local(vel_ref, V, lsem.at[n])
-    n += 1
-    loads["d"] = local(diff_ref, D, lsem.at[n])
+        loads["f", j] = local(gas_ref.at[0, :, pl.ds(128 * j, 128)], FS.at[0, j], lsem.at[4 + j])
+    loads["fl"] = local(flags_ref, FL, lsem.at[6])
+
+    def later_loads():
+        loads["d"] = local(diff_ref, D, lsem.at[7])
+        loads["ow"] = local(owner_ref, OW, lsem.at[8])
+        for f, ref in enumerate((gas_ref, fuel_ref)):
+            for j in range(2):
+                loads["g", f, j] = local(
+                    ref.at[:, :, pl.ds(128 * j, 128)],
+                    G.at[f, pl.ds(1, GL), j, pl.ds(8, 64), :],
+                    lsem.at[9 + 2 * f + j],
+                )
+        loads["v"] = local(vel_ref, V, lsem.at[13])
 
     barrier = pltpu.get_barrier_semaphore()
 
@@ -149,8 +147,10 @@
             self_sends = self_sends + jnp.where(self_, 1, 0)
     count = count + jnp.where(at_wall, 18 - self_sends, 0)
 
-    S[0, NL] = jnp.ones((4, 48, 128), F32)
-    S[1, NL] = jnp.ones((4, 48, 128), F32)
+    SS = (S0, S1)
+    for ref in SS:
+        for k in range(2):
+            ref[NL + k] = jnp.ones((4, 48, 128), F32)
 
     def send(src, dst, ssem, rsem, dev):
         return pltpu.make_async_remote_copy(
@@ -171,8 +171,10 @@
 
     for j in range(4):
         loads["s", j].wait()
+    later_loads()
 
     zero32 = jnp.zeros((32, 128), F32)
+    zero_row = jnp.zeros((1, 128), F32)
 
     def columns(acc, first, last, i, lane):
         both = pltpu.roll(jnp.where(lane < 64, first, last), 2 * i + 1, 1)
@@ -184,9 +186,11 @@
                 i = PU * n + k
                 l = CL * c + i
                 for j in range(4):
-                    WRs[0, 0, j, pl.ds(l, 1), :] = S[0, l, j, 8:9, :]
-                    WRs[0, 1, j, pl.ds(l, 1), :] = S[0, l, j, 39:40, :]
-                acc = columns(acc, S[0, l, 0, 8:40, :], S[0, l, 3, 8:40, :], i, lane32)
+                    S0[l, j, 7:8, :] = zero_row
+                    S0[l, j, 40:41, :] = zero_row
+                    WRs[0, 0, j, pl.ds(l, 1), :] = S0[l, j, 8:9, :]
+                    WRs[0, 1, j, pl.ds(l, 1), :] = S0[l, j, 39:40, :]
+                acc = columns(acc, S0[l, 0, 8:40, :], S0[l, 3, 8:40, :], i, lane32)
             return acc
 
         WCs[0, c] = lax.fori_loop(0, CL // PU, pack, zero32)
@@ -194,10 +198,9 @@
 
     lax.fori_loop(0, CHUNKS, pack_chunk, 0)
 
-    for key in (("g0", 0), ("g0", 1), "fl", ("g1", 0), ("g1", 1)):
+    for key in (("f", 0), ("f", 1), "fl"):
         loads[key].wait()
     for j in range(2):
-        FS[0, j] = G[0, 1, j, 8:72, :]
         FS[1, j] = FL[:, 128 * j : 128 * j + 128].astype(F32)
 
     def gpack(n, acc):
@@ -205,76 +208,16 @@
             l = 2 * n + k
             for f in range(2):
                 for j in range(2):
+                    G[f, l + 1, j, 7:8, :] = zero_row
+                    G[f, l + 1, j, 72:73, :] = zero_row
                     GRs[0, f, j, pl.ds(l, 1), :] = G[f, l + 1, j, 8:9, :]
                     GRs[1, f, j, pl.ds(l, 1), :] = G[f, l + 1, j, 71:72, :]
                 acc = columns(acc, G[f, l + 1, 0, 8:72, :], G[f, l + 1, 1, 8:72, :], f * GL + l, lane64)
         return acc
 
-    GCs[...] = lax.fori_loop(0, GL // 2, gpack, jnp.zeros((64, 128), F32))
-
-    pl.semaphore_wait(barrier, count)
-
-    def face_ref(buf, piece):
-        return buf.at[:, pl.ds(1, 2)] if piece == 0 else buf.at[:, pl.ds(0 if piece == 1 else 3, 1)]
-
-    def face_source(piece):
-        return FS if piece == 0 else FS.at[:, pl.ds(1 if piece == 1 else 0, 1)]
-
-    PART = ((0, 8), (8, 16), (24, 8))
-
-    def face_copy(n, dev, piece, part, r):
-        start, size = PART[part]
-        return send(
-            face_source(piece).at[:, :, pl.ds(r, size), :],
-            face_ref(FB, piece).at[:, :, pl.ds(start, size), :],
-            f_send.at[n],
-            f_recv.at[piece, part],
-            dev,
-        )
-
-    def face_here(piece, part, r):
-        start, size = PART[part]
-        if piece == 0:
-            FB[:, 1:3, start : start + size, :] = FS[:, :, r : r + size, :]
-        elif piece == 1:
-            FB[:, 0, start : start + size, :] = FS[:, 1, r : r + size, :]
-        else:
-            FB[:, 3, start : start + size, :] = FS[:, 0, r : r + size, :]
-
-    g_copies = (
-        send(GRs.at[0], GRr.at[1], g_send.at[0], g_recv.at[1], gxm_dev),
-        send(GRs.at[1], GRr.at[0], g_send.at[1], g_recv.at[0], gxp_dev),
-        send(GCs, GCr.at[1], g_send.at[2], g_recv.at[3], gym_dev),
-        send(GCs, GCr.at[0], g_send.at[3], g_recv.at[2], gyp_dev),
-    )
-    for copy in g_copies:
-        copy.start()
-    for c in range(CHUNKS):
-        for copy in wall_copies(0, c):
-            copy.start()
-
-    @pl.when(at_wall)
-    def _():
-        for n, (dev, piece, part, r, self_) in enumerate(face_targets()):
-            copy = face_copy(n, dev, piece, part, r)
-            if self_ is None:
-                copy.start()
-            else:
-                pl.when(jnp.logical_not(self_))(copy.start)
-                pl.when(self_)(functools.partial(face_here, piece, part, r))
-
-    z_down = send(
-        G.at[:, 1, :, pl.ds(8, 64), :], G.at[:, GL + 1, :, pl.ds(8, 64), :], g_send.at[4], g_recv.at[5], left_dev
-    )
-    z_up = send(
-        G.at[:, GL, :, pl.ds(8, 64), :], G.at[:, 0, :, pl.ds(8, 64), :], g_send.at[5], g_recv.at[4], right_dev
-    )
-    pl.when(jnp.logical_not(at_wall))(z_down.start)
-    pl.when(jnp.logical_not(at_top))(z_up.start)
-
-    def gas_layer(l):
+    def gas_layer(l, inner):
         g = l + 1
-        for f in range(2):
+        for f in range(0 if inner else 2):
             for j in range(2):
                 G[f, g, j, 7:8, :] = GRr[0, f, j, pl.ds(l, 1), :]
                 G[f, g, j, 72:73, :] = GRr[1, f, j, pl.ds(l, 1), :]
@@ -289,7 +232,9 @@
             for f in range(2):
                 i = f * GL + l
                 mid = [G[f, g, j, rows, :] for j in range(2)]
-                edge = pltpu.roll(GC[out, :], lax.bitwise_and(128 - 2 * i, 127), 1)
+                edge = 0.0
+                if not inner:
+                    edge = pltpu.roll(GC[out, :], lax.bitwise_and(128 - 2 * i, 127), 1)
                 lo = [edge] + [pltpu.roll(m, 1, 1) for m in mid]
                 hi = [pltpu.roll(m, 127, 1) for m in mid] + [edge]
                 for j in range(2):
@@ -317,52 +262,186 @@
 
     def gas_layers(first, last):
         def body(l, carry):
-            gas_layer(l)
+            gas_layer(l, True)
             return carry
 
         lax.fori_loop(first, last, body, 0)
 
+    def gas_edges(first, last):
+        def body(n, carry):
+            for k in range(2):
+                l = first + 2 * n + k
+                for f, out, rate in ((0, gas_out, 0.04), (1, fuel_out, 0.03)):
+                    edge = pltpu.roll(GC[...], lax.bitwise_and(128 - 2 * (f * GL + l), 127), 1)
+                    for j in range(2):
+                        lanes = slice(128 * j, 128 * j + 128)
+                        speed = V[1, l, 0:1, lanes]
+                        out[l, 0:1, lanes] = out[l, 0:1, lanes] + (rate + 0.1 * speed) * GRr[0, f, j, pl.ds(l, 1), :]
+                        speed = V[1, l, 63:64, lanes]
+                        out[l, 63:64, lanes] = out[l, 63:64, lanes] + (rate - 0.1 * speed) * GRr[1, f, j, pl.ds(l, 1), :]
+                    speed = V[2, l, :, 0:128]
+                    out[l, :, 0:128] = out[l, :, 0:128] + jnp.where(lane64 == 0, (rate + 0.1 * speed) * edge, 0.0)
+                    speed = V[2, l, :, 128:256]
+                    out[l, :, 128:256] = out[l, :, 128:256] + jnp.where(lane64 == 127, (rate - 0.1 * speed) * edge, 0.0)
+            return carry
+
+        lax.fori_loop(0, (last - first) // 2, body, 0)
+
+    pl.semaphore_wait(barrier, count)
+
+    def face_ref(buf, piece):
+        return buf.at[:, pl.ds(1, 2)] if piece == 0 else buf.at[:, pl.ds(0 if piece == 1 else 3, 1)]
+
+    def face_source(piece):
+        return FS if piece == 0 else FS.at[:, pl.ds(1 if piece == 1 else 0, 1)]
+
+    PART = ((0, 8), (8, 16), (24, 8))
+
+    def face_copy(n, dev, piece, part, r):
+        start, size = PART[part]
+        return send(
+            face_source(piece).at[:, :, pl.ds(r, size), :],
+            face_ref(FB, piece).at[:, :, pl.ds(start, size), :],
+            f_send.at[n],
+            f_recv.at[piece, part],
+            dev,
+        )
+
+    def face_here(piece, part, r):
+        start, size = PART[part]
+        if piece == 0:
+            FB[:, 1:3, start : start + size, :] = FS[:, :, r : r + size, :]
+        elif piece == 1:
+            FB[:, 0, start : start + size, :] = FS[:, 1, r : r + size, :]
+        else:
+            FB[:, 3, start : start + size, :] = FS[:, 0, r : r + size, :]
+
+    g_copies = (
+        send(GRs.at[0], GRr.at[1], g_send.at[0], g_recv.at[1], gxm_dev),
+        send(GRs.at[1], GRr.at[0], g_send.at[1], g_recv.at[0], gxp_dev),
+        send(GCs, GCr.at[1], g_send.at[2], g_recv.at[3], gym_dev),
+        send(GCs, GCr.at[0], g_send.at[3], g_recv.at[2], gyp_dev),
+    )
+    for c in range(CHUNKS):
+        for copy in wall_copies(0, c):
+            copy.start()
+
+    @pl.when(at_wall)
+    def _():
+        for n, (dev, piece, part, r, self_) in enumerate(face_targets()):
+            copy = face_copy(n, dev, piece, part, r)
+            if self_ is None:
+                copy.start()
+            else:
+                pl.when(jnp.logical_not(self_))(copy.start)
+                pl.when(self_)(functools.partial(face_here, piece, part, r))
+
+    z_down = send(
+        G.at[:, 1, :, pl.ds(8, 64), :], G.at[:, GL + 1, :, pl.ds(8, 64), :], g_send.at[4], g_recv.at[5], left_dev
+    )
+    z_up = send(
+        G.at[:, GL, :, pl.ds(8, 64), :], G.at[:, 0, :, pl.ds(8, 64), :], g_send.at[5], g_recv.at[4], right_dev
+    )
+
     def wall_pack(s, c, g, acc):
-        dst = S.at[(s + 1) % 2]
+        dst = SS[(s + 1) % 2]
         for k in range(WU):
             i = WU * g + k
             l = jnp.maximum(CL * c + i, 0)
             acc = columns(acc, dst[l, 0, 8:40, :], dst[l, 3, 8:40, :], i, lane32)
         return acc
 
-    def wall_group(s, c, g, acc):
-        src, dst = S.at[s % 2], S.at[(s + 1) % 2]
-        if s < STEPS - 1:
-            acc = wall_pack(s, c, g - 1, acc)
-        for k in range(WU):
-            i = WU * g + k
+    def wall_sides(s, R, l0):
+        src = SS[s % 2]
+        for k in range(HU):
+            l = l0 + k
+            mid = [src[l, j, 8:40, :] for j in range(4)]
+            lo = [None] + [pltpu.roll(m, 1, 1) for m in mid]
+            hi = [pltpu.roll(m, 127, 1) for m in mid] + [None]
+            for j in range(4):
+                y_lo = lo[j + 1] if j > 0 else jnp.where(lane32 == 0, 0.0, lo[1])
+                y_hi = hi[j] if j < 3 else jnp.where(lane32 == 127, 0.0, hi[3])
+                if j > 0:
+                    y_lo = jnp.where(lane32 == 0, lo[j], y_lo)
+                if j < 3:
+                    y_hi = jnp.where(lane32 == 127, hi[j + 1], y_hi)
+                R[k, j] = y_lo + y_hi
+
+    def wall_half(s, c, i0, R, first, inner=False):
+        src, dst = SS[s % 2], SS[(s + 1) % 2]
+        for k in range(HU):
+            i = i0 + k
             l = CL * c + i
-            for j in range(4):
-                src[l, j, 7:8, :] = WRr[s, 0, j, pl.ds(l, 1), :]
-                src[l, j, 40:41, :] = WRr[s, 1, j, pl.ds(l, 1), :]
-        for k in range(WU):
-            i = WU * g + k
-            l = CL * c + i
-            lm = jnp.maximum(l - 1, 0) if k == 0 else l - 1
-            mid = [src[l, j, 8:40, :] for j in range(4)]
-            edge = pltpu.roll(WC[...], lax.bitwise_and(128 - 2 * i, 127), 1)
-            lo = [edge] + [pltpu.roll(m, 1, 1) for m in mid]
-            hi = [pltpu.roll(m, 127, 1) for m in mid] + [edge]
-            for j in range(4):
-                y_lo = jnp.where(lane32 == 0, lo[j], lo[j + 1])
-                y_hi = jnp.where(lane32 == 127, hi[j + 1], hi[j])
+            lm = jnp.maximum(l - 1, 0) if first and k == 0 else l - 1
+            if not inner:
+                edge = pltpu.roll(WC[...], lax.bitwise_and(128 - 2 * i, 127), 1)
+            for j in (1, 2, 0, 3):
+                mid = src[l, j, 8:40, :]
                 near = (src[lm, j, 8:40, :] + src[l + 1, j, 8:40, :]) + (src[l, j, 7:39, :] + src[l, j, 9:41, :])
-                near = near + (y_lo + y_hi)
+                near = near + R[k, j]
+                if j == 0 and not inner:
+                    near = near + jnp.where(lane32 == 0, edge, 0.0)
+                if j == 3 and not inner:
+                    near = near + jnp.where(lane32 == 127, edge, 0.0)
                 lanes = slice(128 * j, 128 * j + 128)
-                new = mid[j] + D[l, :, lanes] * (near - 6.0 * mid[j])
-                if k == 0:
+                new = mid + D[l, :, lanes] * (near - 6.0 * mid)
+                if first and k == 0 and not inner:
                     new = new + jnp.where(l == 0, FX[j], 0.0)
                 if s == STEPS - 1:
                     solid_out[l, :, lanes] = new
                 else:
                     dst[l, j, 8:40, :] = new
-                    WRs[s + 1, 0, j, pl.ds(l, 1), :] = new[0:1, :]
-                    WRs[s + 1, 1, j, pl.ds(l, 1), :] = new[31:32, :]
+                    if not inner:
+                        WRs[s + 1, 0, j, pl.ds(l, 1), :] = new[0:1, :]
+                        WRs[s + 1, 1, j, pl.ds(l, 1), :] = new[31:32, :]
+
+    def wall_inner():
+        def body(n, carry):
+            wall_sides(0, RB, WU * n + HU)
+            wall_half(0, 0, WU * n, RA, True, True)
+            wall_sides(0, RA, WU * n + WU)
+            wall_half(0, 0, WU * n + HU, RB, False, True)
+            return carry
+
+        wall_sides(0, RA, 0)
+        lax.fori_loop(0, NL // WU, body, 0)
+
+    def wall_edges(c, g, acc):
+        acc = wall_pack(0, c, g - 1, acc)
+        for k in range(WU):
+            i = WU * g + k
+            l = CL * c + i
+            edge = pltpu.roll(WC[...], lax.bitwise_and(128 - 2 * i, 127), 1)
+            for j in (1, 2, 0, 3):
+                lanes = slice(128 * j, 128 * j + 128)
+                top = D[l, 0:1, lanes] * WRr[0, 0, j, pl.ds(l, 1), :]
+                low = D[l, 31:32, lanes] * WRr[0, 1, j, pl.ds(l, 1), :]
+                S1[l, j, 8:9, :] = S1[l, j, 8:9, :] + top
+                S1[l, j, 39:40, :] = S1[l, j, 39:40, :] + low
+                if k == 0:
+                    S1[l, j, 8:40, :] = S1[l, j, 8:40, :] + jnp.where(l == 0, FX[j], 0.0)
+                if j == 0:
+                    S1[l, j, 8:40, :] = S1[l, j, 8:40, :] + jnp.where(lane32 == 0, D[l, :, lanes] * edge, 0.0)
+                if j == 3:
+                    S1[l, j, 8:40, :] = S1[l, j, 8:40, :] + jnp.where(lane32 == 127, D[l, :, lanes] * edge, 0.0)
+                WRs[1, 0, j, pl.ds(l, 1), :] = S1[l, j, 8:9, :]
+                WRs[1, 1, j, pl.ds(l, 1), :] = S1[l, j, 39:40, :]
+        return acc
+
+    def wall_group(s, c, g, acc):
+        src = SS[s % 2]
+        i0 = WU * g
+        if s < STEPS - 1:
+            acc = wall_pack(s, c, g - 1, acc)
+        for k in range(WU):
+            l = CL * c + i0 + k
+            for j in range(4):
+                src[l, j, 7:8, :] = WRr[s, 0, j, pl.ds(l, 1), :]
+                src[l, j, 40:41, :] = WRr[s, 1, j, pl.ds(l, 1), :]
+        wall_sides(s, RB, CL * c + i0 + HU)
+        wall_half(s, c, i0, RA, True)
+        wall_sides(s, RA, CL * c + i0 + WU)
+        wall_half(s, c, i0 + HU, RB, False)
         return acc
 
     def wall_chunk(s, c):
@@ -372,7 +451,7 @@
         WC[...] = jnp.where(even, WCr[s, 0, c], pltpu.roll(WCr[s, 1, c], 126, 1))
 
         def body(g, acc):
-            return wall_group(s, c, g, acc)
+            return wall_edges(c, g, acc) if s == 0 else wall_group(s, c, g, acc)
 
         acc = lax.fori_loop(0, CL // WU, body, zero32)
         if s < STEPS - 1:
@@ -421,22 +500,34 @@
                 value = jnp.where(shift_row == d, picked, value)
             gas_at = jnp.abs(value)
             film = jnp.where(value > 0.0, 0.15 * jnp.exp(0.7 * jnp.log(gas_at)), 0.0)
-            FX[k] = 0.25 * (film * (gas_at - S[0, 0, k, 8:40, :]))
-
+            FX[k] = 0.25 * (film * (gas_at - S0[0, k, 8:40, :]))
+
+    loads["d"].wait()
+    loads["ow"].wait()
+    wall_inner()
+    for f in range(2):
+        for j in range(2):
+            loads["g", f, j].wait()
+    GCs[...] = lax.fori_loop(0, GL // 2, gpack, jnp.zeros((64, 128), F32))
+    for copy in g_copies:
+        copy.start()
+    pl.when(jnp.logical_not(at_wall))(z_down.start)
+    pl.when(jnp.logical_not(at_top))(z_up.start)
     loads["v"].wait()
+    gas_layers(GAS[0], GAS[1])
+    wall_flux()
+    wall_step(0, 0, CHUNKS, False)
+    wall_sides(1, RA, 0)
+    gas_layers(GAS[1], GAS[2])
+    wall_step(1, 0, CHUNKS, False)
+    wall_sides(2, RA, 0)
+    gas_layers(GAS[2], GAS[3])
+    wall_step(2, 0, CHUNKS, False)
+    wall_sides(3, RA, 0)
     for copy in g_copies:
         copy.wait_recv()
     GC[...] = jnp.where(lax.bitwise_and(lane64, 1) == 0, GCr[0], pltpu.roll(GCr[1], 126, 1))
-    gas_layers(1, GAS[0])
-    loads["d"].wait()
-    loads["ow"].wait()
-    wall_flux()
-    wall_step(0, 0, CHUNKS, False)
-    gas_layers(GAS[0], GAS[1])
-    wall_step(1, 0, CHUNKS, False)
-    gas_layers(GAS[1], GAS[2])
-    wall_step(2, 0, CHUNKS, False)
-    gas_layers(GAS[2], GAS[3])
+    gas_edges(EDGES[0], EDGES[1])
     wall_chunk(3, 0)
     for j in range(4):
         T0[j] = solid_out[0, :, 128 * j : 128 * j + 128]
@@ -460,7 +551,7 @@
         WTr[:, 0:16, :] = WTs[...]
 
     wall_step(3, 1, CHUNKS, False)
-    gas_layers(GAS[3], GL - 1)
+    gas_edges(EDGES[1], EDGES[2])
     pl.when(jnp.logical_not(at_top))(z_down.wait_recv)
 
     @pl.when(at_top)
@@ -469,7 +560,7 @@
             for j in range(2):
                 G[f, GL + 1, j, 8:72, :] = G[f, GL, j, 8:72, :]
 
-    gas_layers(GL - 1, GL)
+    gas_layer(GL - 1, False)
 
     @pl.when(jnp.logical_not(at_wall))
     def _():
@@ -486,7 +577,7 @@
             G[0, 0, j, 8:72, :] = jnp.where(FS[1, j] > 0.5, 2.0 * WTr[j] - temp, temp)
             G[1, 0, j, 8:72, :] = G[1, 1, j, 8:72, :]
 
-    gas_layers(0, 1)
+    gas_layer(0, False)
 
     send(WRs.at[:, 0], WRr.at[:, 1], w_send.at[0], w_recv.at[0, 0, 1], up_dev).wait_send()
     send(WRs.at[:, 1], WRr.at[:, 0], w_send.at[1], w_recv.at[0, 0, 0], down_dev).wait_send()
@@ -533,7 +624,8 @@
         scratch_shapes=[
             buf((2, GL + 2, 2, 80, 128), F32),
             buf((3, GL, 64, 256), F32),
-            buf((2, NL + 1, 4, 48, 128), F32),
+            buf((NL + 2, 4, 48, 128), F32),
+            buf((NL + 2, 4, 48, 128), F32),
             buf((NL, 32, 512), F32),
             buf((64, 256), I32),
             buf((32, 512), I32),
@@ -546,6 +638,8 @@
             buf((STEPS, CHUNKS, 32, 128), F32),
             buf((STEPS, 2, CHUNKS, 32, 128), F32),
             buf((32, 128), F32),
+            buf((HU, 4, 32, 128), F32),
+            buf((HU, 4, 32, 128), F32),
             buf((2, 2, 2, GL, 128), F32),
             buf((2, 2, 2, GL, 128), F32),
             buf((64, 128), F32),
@@ -554,7 +648,7 @@
             buf((4, 32, 128), F32),
             buf((2, 16, 128), F32),
             buf((2, 64, 128), F32),
-            dma((12,)),
+            dma((14,)),
             dma((4,)),
             dma((STEPS, CHUNKS, 4)),
             dma((6,)),

time: 54 us -> 52.1 us (0.965)
  Pallas kernels: 53.2 us -> 51.3 us
    pallas_call x1, Pallas kernels: 49.8 us -> 47.9 us  [shards(): pl.pallas_call(kernel, out_shape=[pltpu.VMEM(s, F32) for s in results], i...]
where the time goes in v3:
time: 52.1 us; the launch traced here: 52 us
  Pallas kernels  51.3 us (98%)
  between operations  0.64 us (1%)
    pallas_call x1, Pallas kernels, shards(): pl.pallas_call(kernel, out_shape=[pltpu.VMEM(s, F32) for s in results], i...  47.9 us
    pallas_call x1, Pallas kernels, shards(): pl.pallas_call(writer, out_shape=[jax.ShapeDtypeStruct(s, F32) for s in r...  3.4 us

profile of v3, /device:TPU:1, one launch (start us, length us, event | category | flops | bytes accessed | tf_op | source)
XLA Modules:
  0.0 52.0 jit_solution(14447435217773637410)
XLA Ops:
  0.6 47.9 %section.1 = (f32[32,64,256]{2,1,0:T(8,128)S(1)}, f32[32,64,256]{2,1,0:T(8,128)S(1)}, f32[64,32,512]{2,1,0:T(8,128)S(1)}) custom-call(f32[32,64,256]{2,1,0:T(8,128)} %gas_ref.1, f32[32,64,256]{2,1,0:T(8,128)} %fuel_ref.1, f32[3,32,64,256]{3,2,1,0:T(8,128)} %vel_ref.1, s32[64,256]{1,0:T(8,128)} %flags_ref.1, f32[64,32,512]{2,1,0:T(8,128)} %solid_ref.1, ...), custom_call_target="tpu_custom_call" | custom-call | tf_op jit(solution)/shard_map/section/pallas_call | solution.py:619
  48.6 3.4 %writer.1 = (f32[32,64,256]{2,1,0:T(8,128)}, f32[32,64,256]{2,1,0:T(8,128)}, f32[64,32,512]{2,1,0:T(8,128)}) custom-call(f32[32,64,256]{2,1,0:T(8,128)S(1)} %get-tuple-element.6.a_ref, f32[32,64,256]{2,1,0:T(8,128)S(1)} %get-tuple-element.7.b_ref, f32[64,32,512]{2,1,0:T(8,128)S(1)} %get-tuple-element.8.c_ref), custom_call_target="tpu_custom_call" | custom-call | tf_op jit(solution)/shard_map/writer/pallas_call | solution.py:667

commit v4 on v3

--- a/solution.py
+++ b/solution.py
@@ -18,7 +18,7 @@
 HU = 2
 WU = 2 * HU
 PU = 4
-GAS = (1, 11, 21, 31)
+GAS = (1, 31)
 EDGES = (1, 9, 31)
 GL = 32
 DISP = 4
@@ -322,10 +322,6 @@
         send(GCs, GCr.at[1], g_send.at[2], g_recv.at[3], gym_dev),
         send(GCs, GCr.at[0], g_send.at[3], g_recv.at[2], gyp_dev),
     )
-    for c in range(CHUNKS):
-        for copy in wall_copies(0, c):
-            copy.start()
-
     @pl.when(at_wall)
     def _():
         for n, (dev, piece, part, r, self_) in enumerate(face_targets()):
@@ -335,6 +331,10 @@
             else:
                 pl.when(jnp.logical_not(self_))(copy.start)
                 pl.when(self_)(functools.partial(face_here, piece, part, r))
+
+    for c in range(CHUNKS):
+        for copy in wall_copies(0, c):
+            copy.start()
 
     z_down = send(
         G.at[:, 1, :, pl.ds(8, 64), :], G.at[:, GL + 1, :, pl.ds(8, 64), :], g_send.at[4], g_recv.at[5], left_dev
@@ -518,10 +518,8 @@
     wall_flux()
     wall_step(0, 0, CHUNKS, False)
     wall_sides(1, RA, 0)
-    gas_layers(GAS[1], GAS[2])
     wall_step(1, 0, CHUNKS, False)
     wall_sides(2, RA, 0)
-    gas_layers(GAS[2], GAS[3])
     wall_step(2, 0, CHUNKS, False)
     wall_sides(3, RA, 0)
     for copy in g_copies:

time: 52.1 us -> 49.6 us (0.952)
  Pallas kernels: 51.3 us -> 48.7 us
    pallas_call x1, Pallas kernels: 47.9 us -> 45.3 us  [shards(): pl.pallas_call(kernel, out_shape=[pltpu.VMEM(s, F32) for s in results], i...]
where the time goes in v4:
time: 49.6 us; the launch traced here: 49.3 us
  Pallas kernels  48.7 us (98%)
  between operations  0.64 us (1%)
    pallas_call x1, Pallas kernels, shards(): pl.pallas_call(kernel, out_shape=[pltpu.VMEM(s, F32) for s in results], i...  45.3 us
    pallas_call x1, Pallas kernels, shards(): pl.pallas_call(writer, out_shape=[jax.ShapeDtypeStruct(s, F32) for s in r...  3.4 us

profile of v4, /device:TPU:1, one launch (start us, length us, event | category | flops | bytes accessed | tf_op | source)
XLA Modules:
  0.0 49.3 jit_solution(5799610878563137176)
XLA Ops:
  0.6 45.3 %section.1 = (f32[32,64,256]{2,1,0:T(8,128)S(1)}, f32[32,64,256]{2,1,0:T(8,128)S(1)}, f32[64,32,512]{2,1,0:T(8,128)S(1)}) custom-call(f32[32,64,256]{2,1,0:T(8,128)} %gas_ref.1, f32[32,64,256]{2,1,0:T(8,128)} %fuel_ref.1, f32[3,32,64,256]{3,2,1,0:T(8,128)} %vel_ref.1, s32[64,256]{1,0:T(8,128)} %flags_ref.1, f32[64,32,512]{2,1,0:T(8,128)} %solid_ref.1, ...), custom_call_target="tpu_custom_call" | custom-call | tf_op jit(solution)/shard_map/section/pallas_call | solution.py:617
  45.9 3.4 %writer.1 = (f32[32,64,256]{2,1,0:T(8,128)}, f32[32,64,256]{2,1,0:T(8,128)}, f32[64,32,512]{2,1,0:T(8,128)}) custom-call(f32[32,64,256]{2,1,0:T(8,128)S(1)} %get-tuple-element.6.a_ref, f32[32,64,256]{2,1,0:T(8,128)S(1)} %get-tuple-element.7.b_ref, f32[64,32,512]{2,1,0:T(8,128)S(1)} %get-tuple-element.8.c_ref), custom_call_target="tpu_custom_call" | custom-call | tf_op jit(solution)/shard_map/writer/pallas_call | solution.py:665
